TPU v7x, 32 devices: a whole 2x2x4 slice. The times are simulated.
32 devices in a mesh: aux: 4 (over y, x), pair: 8 (over z, core).
Axes of the slice: x: 2, y: 2, z: 4, core: 2. Of those that a mesh axis runs over, the one named last changes fastest.
Arguments:
- m_panels: bfloat16 [40000, 8192], P('aux', 'pair'), may hold values from -6 to 6
- lower_cols: bfloat16 [2, 512, 40000], P(None, 'pair', 'aux'), may hold values from -0.2 to 0.2, as said below
- diag_inverses: float32 [2, 512, 512], replicated, may hold values from -0.2 to 2, as said below
Outputs:
- remainder: bfloat16 [40000, 8192], P('aux', 'pair')
- solved: bfloat16 [2, 512, 8192], P(None, None, 'pair')
Inputs may be any that keep to these rules, and one draw needn't show every extreme that they name: lower_cols[k] is zero in the pivot rows of panels 0 to k (the factor is lower triangular and its diagonal blocks are given by their inverses). Each diag_inverses[k] is lower triangular.
All inputs are finite; a program needn't handle non-finite values.
Results may differ from a plain program's by a relative error of at most 0.0047.
Values may be sent and summed in bfloat16 or wider, within the bound.
A program may use at most 192 MiB of HBM per device.

v0:
```python
import functools

import jax
import jax.numpy as jnp
from jax import lax
from jax.experimental import pallas as pl
from jax.experimental.pallas import tpu as pltpu
from jax.sharding import PartitionSpec as P

CHUNKS = 10
TILE = 256
CORES = 2
CONTRACT = (((0,), (0,)), ((), ()))
MESH = pl.DeviceIdType.MESH


def kernel(aux, chips, chunks, chunk, m_hbm, l_hbm, l_tail, dinv_ref, mbuf, solved_ref,
           lbuf, sbuf, load_sem, ring_sem, swap_sem, left_sem, right_sem, part_sem,
           srecv_sem, ssend_sem):
    rows, columns = m_hbm.shape
    panels, width = dinv_ref.shape[:2]
    even = rows - rows % TILE
    padded = lbuf.shape[-1]
    a = lax.axis_index("aux")
    me = lax.axis_index("pair")
    z, c = me // CORES, lax.rem(me, CORES)
    to_left = {"pair": lax.rem(z + chips - 1, chips) * CORES + c}
    to_right = {"pair": lax.rem(z + 1, chips) * CORES + c}
    partner = {"pair": z * CORES + 1 - c}

    own_load = pltpu.make_async_copy(
        l_hbm.at[:, :, pl.ds(0, even)], lbuf.at[me, :, :, pl.ds(0, even)], load_sem.at[0])
    own_tail = pltpu.make_async_copy(
        l_tail, lbuf.at[me, :, :, pl.ds(even, padded - even)], load_sem.at[3])
    pivot_load = pltpu.make_async_copy(
        m_hbm.at[pl.ds(0, width)], mbuf.at[pl.ds(0, width)], load_sem.at[1])
    rest_load = pltpu.make_async_copy(
        m_hbm.at[pl.ds(width, rows - width)], mbuf.at[pl.ds(width, rows - width)], load_sem.at[2])
    own_load.start()
    own_tail.start()
    pivot_load.start()

    barrier = pltpu.get_barrier_semaphore()
    for peer in (to_left, to_right, partner):
        pl.semaphore_signal(barrier, inc=1, device_id=peer, device_id_type=MESH)
    for step in range(1, aux):
        peer = {"aux": lax.rem(a + step, aux)}
        pl.semaphore_signal(barrier, inc=1, device_id=peer, device_id_type=MESH)
    pl.semaphore_wait(barrier, 2 + aux)
    own_load.wait()
    own_tail.wait()
    rest_load.start()

    def piece(block, j):
        return lbuf.at[block, :, :, pl.ds(pl.multiple_of(j * chunk, 128), chunk)]

    def ring(zb, j, send, peer):
        ref = piece(zb * CORES + c, j)
        return pltpu.make_async_remote_copy(
            src_ref=ref, dst_ref=ref, send_sem=send.at[zb, j], recv_sem=ring_sem.at[zb, j],
            device_id=peer, device_id_type=MESH)

    def swap(zb, j, core):
        ref = piece(zb * CORES + core, j)
        return pltpu.make_async_remote_copy(
            src_ref=ref, dst_ref=ref, send_sem=part_sem.at[zb, j], recv_sem=swap_sem.at[zb, j],
            device_id=partner, device_id_type=MESH)

    def solve(panel):
        def columns_of(i, _):
            cols = pl.ds(pl.multiple_of(i * TILE, TILE), TILE)
            pivot = mbuf[pl.ds(0, width), cols].astype(jnp.float32)
            for before in range(panel):
                factor = lbuf[:, before, :, pl.ds(0, width)].reshape(-1, width)
                pivot = pivot - lax.dot_general(
                    factor, sbuf[before, :, cols], CONTRACT, preferred_element_type=jnp.float32)
            sbuf[panel, :, cols] = jnp.dot(
                dinv_ref[panel], pivot, precision=lax.Precision.HIGHEST,
                preferred_element_type=jnp.float32).astype(jnp.bfloat16)
            return 0

        lax.fori_loop(0, columns // TILE, columns_of, 0)

    def spread(panel, step):
        return pltpu.make_async_remote_copy(
            src_ref=sbuf.at[panel], dst_ref=sbuf.at[panel],
            send_sem=ssend_sem.at[panel, step], recv_sem=srecv_sem.at[panel],
            device_id={"aux": lax.rem(a + step, aux)}, device_id_type=MESH)

    def settle(panel):
        solve(panel)
        for step in range(1, aux):
            spread(panel, step).start()

    def product(here):
        return sum(
            lax.dot_general(
                lbuf[:, panel, :, here].reshape(-1, TILE), sbuf[panel], CONTRACT,
                preferred_element_type=jnp.float32)
            for panel in range(panels))

    def update(j):
        def tile(i, _):
            here = pl.ds(pl.multiple_of(i * TILE, TILE), TILE)
            mbuf[here] = (mbuf[here].astype(jnp.float32) - product(here)).astype(jnp.bfloat16)
            return 0

        tiles = chunk // TILE
        lax.fori_loop(j * tiles, jnp.minimum((j + 1) * tiles, even // TILE), tile, 0)

    def complete(j):
        for zb in range(chips):
            swap(zb, j, 1 - c).wait_recv()

    def tick(t):
        @pl.when(t < chunks)
        def _():
            @pl.when(z > 0)
            def _():
                ring(z, t, left_sem, to_left).start()

            @pl.when(z < chips - 1)
            def _():
                ring(z, t, right_sem, to_right).start()

            swap(z, t, c).start()

        for step in range(1, chips):
            j = t - step
            live = jnp.logical_and(j >= 0, j < chunks)

            @pl.when(jnp.logical_and(live, z + step < chips))
            def _():
                ring(z + step, j, left_sem, to_left).wait_recv()

                @pl.when(z > 0)
                def _():
                    ring(z + step, j, left_sem, to_left).start()

                swap(z + step, j, c).start()

            @pl.when(jnp.logical_and(live, z >= step))
            def _():
                ring(z - step, j, right_sem, to_right).wait_recv()

                @pl.when(z < chips - 1)
                def _():
                    ring(z - step, j, right_sem, to_right).start()

                swap(z - step, j, c).start()

        j = t - (chips - 1)

        @pl.when(jnp.logical_and(j >= 0, j < chunks))
        def _():
            complete(j)

    first = max(chips + panels, chunks // 2 + chips)
    last = chunks + chips - 1

    def ticks(t, _):
        tick(t)
        return 0

    tick(jnp.int32(0))
    pivot_load.wait()

    @pl.when(a == 0)
    def _():
        settle(0)

    lax.fori_loop(1, chips, ticks, 0)
    for panel in range(1, panels):
        @pl.when(a == panel)
        def _(panel=panel):
            for before in range(panel):
                spread(before, 1).wait_recv()
            settle(panel)

        lax.fori_loop(chips - 1 + panel, chips + panel, ticks, 0)
    lax.fori_loop(chips - 1 + panels, first, ticks, 0)

    for panel in range(panels):
        @pl.when(jnp.logical_and(a != panel, jnp.logical_or(a < panel, a >= panels)))
        def _(panel=panel):
            spread(panel, 1).wait_recv()
    rest_load.wait()
    solved_ref[...] = sbuf[...]

    def updates(j, _):
        update(j)
        return 0

    lax.fori_loop(0, first - chips + 1, updates, 0)

    def both(t, _):
        tick(t)
        update(t - (chips - 1))
        return 0

    lax.fori_loop(first, last, both, 0)

    if even < rows:
        left = rows - even
        here = pl.ds(even, left)
        total = mbuf[here].astype(jnp.float32) - product(pl.ds(even, TILE))[:left]
        mbuf[here] = total.astype(jnp.bfloat16)

    def drain(j, _):
        for zb in range(chips):
            @pl.when(jnp.logical_and(z > 0, z <= zb))
            def _():
                ring(jnp.int32(zb), j, left_sem, to_left).wait_send()

            @pl.when(jnp.logical_and(z < chips - 1, z >= zb))
            def _():
                ring(jnp.int32(zb), j, right_sem, to_right).wait_send()

            swap(jnp.int32(zb), j, c).wait_send()
        return 0

    lax.fori_loop(0, chunks, drain, 0)
    for panel in range(panels):
        @pl.when(a == panel)
        def _(panel=panel):
            for step in range(1, aux):
                spread(panel, step).wait_send()


def shards(aux, pair, m_panels, lower_cols, diag_inverses):
    panels, width = diag_inverses.shape[:2]
    rows, columns = m_panels.shape
    part = lower_cols.shape[1]
    chips = pair // CORES
    chunk = max(-(-rows // (CHUNKS * TILE)), -(-width // TILE)) * TILE
    chunks = -(-rows // chunk)
    padded = chunks * chunk
    even = rows - rows % TILE
    tail = jnp.pad(lower_cols[:, :, even:], ((0, 0), (0, 0), (0, padded - rows)))
    anywhere = pl.BlockSpec(memory_space=pl.ANY)
    vmem = pl.BlockSpec(memory_space=pltpu.VMEM)
    dma = pltpu.SemaphoreType.DMA
    return pl.pallas_call(
        functools.partial(kernel, aux, chips, chunks, chunk),
        in_specs=[anywhere, anywhere, anywhere, vmem],
        out_specs=[vmem, vmem],
        out_shape=[
            pltpu.VMEM((rows, columns), jnp.bfloat16),
            jax.ShapeDtypeStruct((panels, width, columns), jnp.bfloat16),
        ],
        scratch_shapes=[
            pltpu.VMEM((pair, panels, part, padded), jnp.bfloat16),
            pltpu.VMEM((panels, width, columns), jnp.bfloat16),
            dma((4,)),
            dma((chips, chunks)),
            dma((chips, chunks)),
            dma((chips, chunks)),
            dma((chips, chunks)),
            dma((chips, chunks)),
            dma((panels,)),
            dma((panels, aux)),
        ],
        compiler_params=pltpu.CompilerParams(
            collective_id=0, has_side_effects=True, vmem_limit_bytes=40 * 1024 * 1024),
    )(m_panels, lower_cols, tail, diag_inverses)


def solution(mesh):
    placed = (P("aux", "pair"), P(None, "pair", "aux"), P())
    return jax.shard_map(
        functools.partial(shards, mesh.shape["aux"], mesh.shape["pair"]),
        mesh=mesh,
        in_specs=placed,
        out_specs=(P("aux", "pair"), P(None, None, "pair")),
        check_vma=False,
    )
```

profile of v0, /device:TPU:3, one launch (start us, length us, event | category | flops | bytes accessed | tf_op | source)
XLA Modules:
  0.0 193.1 jit_solution(16273460914320475264)
XLA Ops:
  0.6 0.8 slice.3
  1.4 0.6 pad.4.l_tail
  2.0 182.3 %shard_map.50 = (bf16[10000,1024]{1,0:T(8,128)(2,1)S(1)}, bf16[2,512,1024]{2,1,0:T(8,128)(2,1)}) custom-call(bf16[10000,1024]{1,0:T(8,128)(2,1)} %m_hbm.1, bf16[2,64,10000]{2,1,0:T(8,128)(2,1)} %l_hbm.1, bf16[2,64,256]{2,1,0:T(8,128)(2,1)} %pad.4.l_tail, f32[2,512,512]{2,1,0:T(8,128)} %dinv_ref.1), custom_call_target="tpu_custom_call" | custom-call | tf_op jit(solution)/shard_map/pallas_call | solution.py:243
  184.3 0.0 copy-start
  184.3 7.5 %copy.7 = bf16[10000,1024]{1,0:T(8,128)(2,1)} copy(bf16[10000,1024]{1,0:T(8,128)(2,1)S(1)} %get-tuple-element.2) | data formatting | bytes 40960000
  191.8 0.0 copy-done
  191.8 1.3 copy.8
Async XLA Ops:
  184.3 7.5 %copy-start = (bf16[2,512,1024]{2,1,0:T(8,128)(2,1)S(1)}, bf16[2,512,1024]{2,1,0:T(8,128)(2,1)}, u32[]{:S(2)}) copy-start(bf16[2,512,1024]{2,1,0:T(8,128)(2,1)} %get-tuple-element.7) | copy-start | bytes 6291460
where the time goes:
time: 195 us; the launch traced here: 193 us
  Pallas kernels  182 us (93%)
  local copies, waits for them, and re-layouts  10.2 us (5%)
    pallas_call x1, Pallas kernels, shards(): pl.pallas_call(functools.partial(kernel, aux, chips, chunks, chunk), in_s...  182 us
    unnamed x4, local copies, waits for them, and re-layouts  8.82 us

commit v1 on v0

v1 whole, which is shorter than its diff:
```python
import functools

import jax
import jax.numpy as jnp
from jax import lax
from jax.experimental import pallas as pl
from jax.experimental.pallas import tpu as pltpu
from jax.sharding import PartitionSpec as P

CHUNK = 1024
TILE = 256
LANES = 128
CORES = 2
WINDOW = 2
CONTRACT = (((0,), (0,)), ((), ()))
MESH = pl.DeviceIdType.MESH


def gather_kernel(aux, chips, chunk, m_hbm, l_hbm, d_hbm, mbuf, sbuf, ltail,
                  lbuf, ebuf, dbuf, load_sem, ring_sem, swap_sem, left_sem, right_sem, part_sem,
                  srecv_sem, ssend_sem):
    rows, columns = m_hbm.shape
    panels, width = d_hbm.shape[:2]
    whole = lbuf.shape[-1]
    mains = whole // chunk
    tail = ltail.shape[-1]
    pieces = mains + 1
    a = lax.axis_index("aux")
    me = lax.axis_index("pair")
    z, c = me // CORES, lax.rem(me, CORES)
    to_left = {"pair": lax.rem(z + chips - 1, chips) * CORES + c}
    to_right = {"pair": lax.rem(z + 1, chips) * CORES + c}
    partner = {"pair": z * CORES + 1 - c}

    def local(src, dst, i):
        return pltpu.make_async_copy(src, dst, load_sem.at[i])

    head_load = local(l_hbm.at[:, :, pl.ds(0, chunk)], lbuf.at[me, :, :, pl.ds(0, chunk)], 0)
    body_load = local(l_hbm.at[:, :, pl.ds(chunk, whole - chunk)],
                      lbuf.at[me, :, :, pl.ds(chunk, whole - chunk)], 1)
    tail_load = local(l_hbm.at[:, :, pl.ds(whole, rows - whole)], ebuf, 2)
    pivot_load = local(m_hbm.at[pl.ds(0, width)], mbuf.at[pl.ds(0, width)], 3)
    rest_load = local(m_hbm.at[pl.ds(width, rows - width)],
                      mbuf.at[pl.ds(width, rows - width)], 4)
    inverse_load = local(d_hbm, dbuf, 5)
    head_load.start()

    barrier = pltpu.get_barrier_semaphore()
    for peer in (to_left, to_right, partner):
        pl.semaphore_signal(barrier, inc=1, device_id=peer, device_id_type=MESH)
    for step in range(1, aux):
        peer = {"aux": lax.rem(a + step, aux)}
        pl.semaphore_signal(barrier, inc=1, device_id=peer, device_id_type=MESH)
    body_load.start()
    tail_load.start()
    pivot_load.start()
    inverse_load.start()
    pl.semaphore_wait(barrier, 2 + aux)
    head_load.wait()

    def piece(block, j, size):
        if size == chunk:
            return lbuf.at[block, :, :, pl.ds(pl.multiple_of(j * chunk, LANES), chunk)]
        return ltail.at[block]

    def ring(zb, j, size, send, peer):
        ref = piece(zb * CORES + c, j, size)
        return pltpu.make_async_remote_copy(
            src_ref=ref, dst_ref=ref, send_sem=send.at[zb, j], recv_sem=ring_sem.at[zb, j],
            device_id=peer, device_id_type=MESH)

    def swap(zb, j, size, core):
        ref = piece(zb * CORES + core, j, size)
        return pltpu.make_async_remote_copy(
            src_ref=ref, dst_ref=ref, send_sem=part_sem.at[zb, j], recv_sem=swap_sem.at[zb, j],
            device_id=partner, device_id_type=MESH)

    def sized(j, act):
        @pl.when(jnp.logical_and(j >= 0, j < mains))
        def _():
            act(j, chunk)

        @pl.when(j == mains)
        def _():
            act(mains, tail)

    def send(zb, j, size, leftward, rightward):
        @pl.when(jnp.logical_and(leftward, z > 0))
        def _():
            ring(zb, j, size, left_sem, to_left).start()

        @pl.when(jnp.logical_and(rightward, z < chips - 1))
        def _():
            ring(zb, j, size, right_sem, to_right).start()

        swap(zb, j, size, c).start()

    def sent(zb, j, size, leftward, rightward):
        @pl.when(jnp.logical_and(leftward, z > 0))
        def _():
            ring(zb, j, size, left_sem, to_left).wait_send()

        @pl.when(jnp.logical_and(rightward, z < chips - 1))
        def _():
            ring(zb, j, size, right_sem, to_right).wait_send()

        swap(zb, j, size, c).wait_send()

    def own(j, size):
        send(z, j, size, True, True)

    def own_sent(j, size):
        sent(z, j, size, True, True)

    def pass_on(step, j, size):
        @pl.when(z + step < chips)
        def _():
            ring(z + step, j, size, left_sem, to_left).wait_recv()
            send(z + step, j, size, True, False)

        @pl.when(z >= step)
        def _():
            ring(z - step, j, size, right_sem, to_right).wait_recv()
            send(z - step, j, size, False, True)

    def passed(step, j, size):
        @pl.when(z + step < chips)
        def _():
            sent(z + step, j, size, True, False)

        @pl.when(z >= step)
        def _():
            sent(z - step, j, size, False, True)

    def complete(j, size):
        for zb in range(chips):
            swap(zb, j, size, 1 - c).wait_recv()

    def solve(panel):
        def columns_of(i, _):
            cols = pl.ds(pl.multiple_of(i * TILE, TILE), TILE)
            pivot = mbuf[pl.ds(0, width), cols].astype(jnp.float32)
            for before in range(panel):
                factor = lbuf[:, before, :, pl.ds(0, width)].reshape(-1, width)
                pivot = pivot - lax.dot_general(
                    factor, sbuf[before, :, cols], CONTRACT, preferred_element_type=jnp.float32)
            sbuf[panel, :, cols] = jnp.dot(
                dbuf[panel], pivot, precision=lax.Precision.HIGHEST,
                preferred_element_type=jnp.float32).astype(jnp.bfloat16)
            return 0

        lax.fori_loop(0, columns // TILE, columns_of, 0)

    def spread(panel, step):
        return pltpu.make_async_remote_copy(
            src_ref=sbuf.at[panel], dst_ref=sbuf.at[panel],
            send_sem=ssend_sem.at[panel, step], recv_sem=srecv_sem.at[panel],
            device_id={"aux": lax.rem(a + step, aux)}, device_id_type=MESH)

    def settle(panel):
        solve(panel)
        for step in range(1, aux):
            spread(panel, step).start()

    def update(j, _):
        def tile(i, _):
            here = pl.ds(pl.multiple_of(i * TILE, TILE), TILE)
            product = sum(
                lax.dot_general(
                    lbuf[:, panel, :, here].reshape(-1, TILE), sbuf[panel], CONTRACT,
                    preferred_element_type=jnp.float32)
                for panel in range(panels))
            mbuf[here] = (mbuf[here].astype(jnp.float32) - product).astype(jnp.bfloat16)
            return 0

        tiles = chunk // TILE
        lax.fori_loop(j * tiles, (j + 1) * tiles, tile, 0)
        return 0

    last = pieces + chips
    first = min(chips + panels + 1, last - 1 - (mains + 1) // 2)

    def done_by(t):
        ready = jnp.minimum(t - chips + 1, 2 * (t - first + 1))
        return jnp.clip(jnp.where(t == last - 1, mains, ready), 0, mains)

    def tick(t, _):
        sized(t - WINDOW, own_sent)
        sized(t, own)
        sized(t - chips, complete)

        for panel in range(1, panels):
            @pl.when(jnp.logical_and(t == chips - 1 + panel, a == panel))
            def _(panel=panel):
                for before in range(panel):
                    spread(before, 1).wait_recv()
                settle(panel)

        @pl.when(t == first)
        def _():
            rest_load.wait()
            for panel in range(panels):
                @pl.when(jnp.logical_and(a != panel, jnp.logical_or(a < panel, a >= panels)))
                def _(panel=panel):
                    spread(panel, 1).wait_recv()

        lax.fori_loop(done_by(t - 1), done_by(t), update, 0)
        for step in range(1, chips):
            sized(t - WINDOW - step, functools.partial(passed, step))
            sized(t - step, functools.partial(pass_on, step))
        return 0

    own(jnp.int32(0), chunk)
    body_load.wait()
    tail_load.wait()
    rest_load.start()
    ltail[me, :, :, pl.ds(0, rows - whole)] = ebuf[...]
    own(jnp.int32(1), chunk)
    pivot_load.wait()
    inverse_load.wait()

    @pl.when(a == 0)
    def _():
        settle(0)

    for step in range(1, chips):
        sized(jnp.int32(1 - step), functools.partial(pass_on, step))
    lax.fori_loop(2, last, tick, 0)

    def drain(t, _):
        sized(t - WINDOW, own_sent)
        for step in range(1, chips):
            sized(t - WINDOW - step, functools.partial(passed, step))
        return 0

    lax.fori_loop(last, last + WINDOW, drain, 0)
    for panel in range(panels):
        @pl.when(a == panel)
        def _(panel=panel):
            for step in range(1, aux):
                spread(panel, step).wait_send()


def write_kernel(chunk, mbuf, sbuf, ltail, out_hbm, solved_hbm, tbuf, out_sem, tail_sem, s_sem):
    rows = mbuf.shape[0]
    panels = sbuf.shape[0]
    mains = out_sem.shape[0]
    whole = mains * chunk

    def main(j):
        here = pl.ds(pl.multiple_of(j * chunk, chunk), chunk)
        return pltpu.make_async_copy(mbuf.at[here], out_hbm.at[here], out_sem.at[j])

    lax.fori_loop(0, mains, lambda j, _: (main(j).start(), 0)[1], 0)
    solved = pltpu.make_async_copy(sbuf, solved_hbm, s_sem)
    solved.start()

    def product(here, size):
        return sum(
            lax.dot_general(
                ltail[:, panel, :, here].reshape(-1, size), sbuf[panel], CONTRACT,
                preferred_element_type=jnp.float32)
            for panel in range(panels))

    left = rows - whole
    full = left // TILE
    for i in range(full):
        here = pl.ds(i * TILE, TILE)
        total = mbuf[pl.ds(whole + i * TILE, TILE)].astype(jnp.float32) - product(here, TILE)
        tbuf[here] = total.astype(jnp.bfloat16)
    if left % TILE:
        here = pl.ds(full * TILE, left % TILE)
        size = min(-(-(left % TILE) // LANES) * LANES, ltail.shape[-1] - full * TILE)
        total = product(pl.ds(full * TILE, size), size)[:left % TILE]
        total = mbuf[pl.ds(whole + full * TILE, left % TILE)].astype(jnp.float32) - total
        tbuf[here] = total.astype(jnp.bfloat16)
    final = pltpu.make_async_copy(tbuf, out_hbm.at[pl.ds(whole, left)], tail_sem)
    lax.fori_loop(0, mains, lambda j, _: (main(j).wait(), 0)[1], 0)
    final.start()
    solved.wait()
    final.wait()


def shards(aux, pair, m_panels, lower_cols, diag_inverses):
    panels, width = diag_inverses.shape[:2]
    rows, columns = m_panels.shape
    part = lower_cols.shape[1]
    chips = pair // CORES
    padded = -(-rows // LANES) * LANES
    chunk = max(CHUNK, -(-width // TILE) * TILE)
    mains = (rows - 1) // chunk
    tail = padded - mains * chunk
    pieces = mains + 1
    anywhere = pl.BlockSpec(memory_space=pl.ANY)
    vmem = pl.BlockSpec(memory_space=pltpu.VMEM)
    dma = pltpu.SemaphoreType.DMA
    held, solved, ltail = pl.pallas_call(
        functools.partial(gather_kernel, aux, chips, chunk),
        in_specs=[anywhere, anywhere, anywhere],
        out_specs=[vmem, vmem, vmem],
        out_shape=[
            pltpu.VMEM((rows, columns), jnp.bfloat16),
            pltpu.VMEM((panels, width, columns), jnp.bfloat16),
            pltpu.VMEM((pair, panels, part, tail), jnp.bfloat16),
        ],
        scratch_shapes=[
            pltpu.VMEM((pair, panels, part, mains * chunk), jnp.bfloat16),
            pltpu.VMEM((panels, part, rows - mains * chunk), jnp.bfloat16),
            pltpu.VMEM((panels, width, width), jnp.float32),
            dma((6,)),
            dma((chips, pieces)),
            dma((chips, pieces)),
            dma((chips, pieces)),
            dma((chips, pieces)),
            dma((chips, pieces)),
            dma((panels,)),
            dma((panels, aux)),
        ],
        compiler_params=pltpu.CompilerParams(
            collective_id=0, has_side_effects=True, vmem_limit_bytes=36 * 1024 * 1024),
    )(m_panels, lower_cols, diag_inverses)
    return pl.pallas_call(
        functools.partial(write_kernel, chunk),
        in_specs=[vmem, vmem, vmem],
        out_specs=[anywhere, anywhere],
        out_shape=[
            jax.ShapeDtypeStruct((rows, columns), jnp.bfloat16),
            jax.ShapeDtypeStruct((panels, width, columns), jnp.bfloat16),
        ],
        scratch_shapes=[
            pltpu.VMEM((rows - mains * chunk, columns), jnp.bfloat16),
            dma((mains,)),
            dma,
            dma,
        ],
        compiler_params=pltpu.CompilerParams(vmem_limit_bytes=8 * 1024 * 1024),
    )(held, solved, ltail)


def solution(mesh):
    placed = (P("aux", "pair"), P(None, "pair", "aux"), P())
    return jax.shard_map(
        functools.partial(shards, mesh.shape["aux"], mesh.shape["pair"]),
        mesh=mesh,
        in_specs=placed,
        out_specs=(P("aux", "pair"), P(None, None, "pair")),
        check_vma=False,
    )
```

time: 195 us -> 185 us (0.949)
  local copies, waits for them, and re-layouts: 10.2 us -> 0 us
    unnamed x4 -> x0, local copies, waits for them, and re-layouts: 8.82 us -> none
    pallas_call x1 -> x2, Pallas kernels: 182 us -> 182 us  [the longest x1 174 us: shards(): pl.pallas_call(functools.partial(gather_kernel, aux, chips, chunk), in_sp...]
where the time goes in v1:
time: 185 us; the launch traced here: 183 us
  Pallas kernels  182 us (98%)
    pallas_call x1, Pallas kernels, shards(): pl.pallas_call(functools.partial(gather_kernel, aux, chips, chunk), in_sp...  174 us
    pallas_call x1, Pallas kernels, shards(): pl.pallas_call(functools.partial(write_kernel, chunk), in_specs=[vmem, vm...  7.73 us

profile of v1, /device:TPU:3, one launch (start us, length us, event | category | flops | bytes accessed | tf_op | source)
XLA Modules:
  0.0 182.6 jit_solution(17362926573663956981)
XLA Ops:
  0.6 174.2 %shard_map.50 = (bf16[10000,1024]{1,0:T(8,128)(2,1)S(1)}, bf16[2,512,1024]{2,1,0:T(8,128)(2,1)S(1)}, bf16[8,2,64,896]{3,2,1,0:T(8,128)(2,1)S(1)}) custom-call(bf16[10000,1024]{1,0:T(8,128)(2,1)} %m_hbm.1, bf16[2,64,10000]{2,1,0:T(8,128)(2,1)} %l_hbm.1, f32[2,512,512]{2,1,0:T(8,128)} %d_hbm.1), custom_call_target="tpu_custom_call" | custom-call | tf_op jit(solution)/shard_map/pallas_call | solution.py:297
  174.8 7.7 %shard_map.51 = (bf16[10000,1024]{1,0:T(8,128)(2,1)}, bf16[2,512,1024]{2,1,0:T(8,128)(2,1)}) custom-call(bf16[10000,1024]{1,0:T(8,128)(2,1)S(1)} %get-tuple-element.5.mbuf, bf16[2,512,1024]{2,1,0:T(8,128)(2,1)S(1)} %get-tuple-element.6.sbuf, bf16[8,2,64,896]{3,2,1,0:T(8,128)(2,1)S(1)} %get-tuple-element.7.ltail), custom_call_target="tpu_custom_call" | custom-call | tf_op jit(solution)/shard_map/pallas_call | solution.py:322

commit v2 on v1

--- a/solution.py
+++ b/solution.py
@@ -8,12 +8,58 @@
 from jax.sharding import PartitionSpec as P
 
 CHUNK = 1024
+LATE = 1
 TILE = 256
 LANES = 128
+SUBLANES = 16
 CORES = 2
 WINDOW = 2
 CONTRACT = (((0,), (0,)), ((), ()))
 MESH = pl.DeviceIdType.MESH
+
+
+def packing(left, groups):
+    ragged = left % LANES
+    return left // LANES, ragged, LANES // ragged if ragged else groups
+
+
+def tail_rows(panels, part, left):
+    groups = panels * part // SUBLANES
+    tiles, ragged, fit = packing(left, groups)
+    return panels * tiles * part + (-(-groups // fit) * SUBLANES if ragged else 0)
+
+
+def late_pieces(chunk, panels, part, left):
+    tiles = left // LANES
+    cuts = {0, max(0, tiles - TILE // LANES)}
+    for k in range(1, LATE + 1):
+        cuts.add(min(k * (chunk // LANES), tiles))
+    cuts = sorted(cuts)
+    starts = [cut * panels * part for cut in cuts]
+    ends = starts[1:] + [tail_rows(panels, part, left)]
+    return [(start, end - start) for start, end in zip(starts, ends) if end > start]
+
+
+def pack(ebuf, ltail, me):
+    panels, part, left = ebuf.shape
+    groups = panels * part // SUBLANES
+    tiles, ragged, fit = packing(left, groups)
+    for panel in range(panels):
+        for i in range(tiles):
+            at = (i * panels + panel) * part
+            ltail[me, pl.ds(at, part)] = ebuf[panel, :, pl.ds(i * LANES, LANES)]
+    if not ragged:
+        return
+    base = panels * tiles * part
+    end = ebuf[:, :, pl.ds(tiles * LANES, ragged)].reshape(groups, SUBLANES, ragged)
+    row = lax.broadcasted_iota(jnp.int32, (ragged, LANES), 0)
+    lane = lax.broadcasted_iota(jnp.int32, (ragged, LANES), 1)
+    for slot in range(-(-groups // fit)):
+        total = jnp.zeros((SUBLANES, LANES), jnp.float32)
+        for g in range(slot * fit, min(groups, (slot + 1) * fit)):
+            place = (lane == row + (g - slot * fit) * ragged).astype(jnp.bfloat16)
+            total = total + jnp.dot(end[g], place, preferred_element_type=jnp.float32)
+        ltail[me, pl.ds(base + slot * SUBLANES, SUBLANES)] = total.astype(jnp.bfloat16)
 
 
 def gather_kernel(aux, chips, chunk, m_hbm, l_hbm, d_hbm, mbuf, sbuf, ltail,
@@ -23,8 +69,9 @@
     panels, width = d_hbm.shape[:2]
     whole = lbuf.shape[-1]
     mains = whole // chunk
-    tail = ltail.shape[-1]
-    pieces = mains + 1
+    left = rows - whole
+    late = late_pieces(chunk, panels, l_hbm.shape[1], left)
+    pieces = mains + len(late)
     a = lax.axis_index("aux")
     me = lax.axis_index("pair")
     z, c = me // CORES, lax.rem(me, CORES)
@@ -38,7 +85,7 @@
     head_load = local(l_hbm.at[:, :, pl.ds(0, chunk)], lbuf.at[me, :, :, pl.ds(0, chunk)], 0)
     body_load = local(l_hbm.at[:, :, pl.ds(chunk, whole - chunk)],
                       lbuf.at[me, :, :, pl.ds(chunk, whole - chunk)], 1)
-    tail_load = local(l_hbm.at[:, :, pl.ds(whole, rows - whole)], ebuf, 2)
+    tail_load = local(l_hbm.at[:, :, pl.ds(whole, left)], ebuf, 2)
     pivot_load = local(m_hbm.at[pl.ds(0, width)], mbuf.at[pl.ds(0, width)], 3)
     rest_load = local(m_hbm.at[pl.ds(width, rows - width)],
                       mbuf.at[pl.ds(width, rows - width)], 4)
@@ -61,7 +108,7 @@
     def piece(block, j, size):
         if size == chunk:
             return lbuf.at[block, :, :, pl.ds(pl.multiple_of(j * chunk, LANES), chunk)]
-        return ltail.at[block]
+        return ltail.at[block, pl.ds(*size)]
 
     def ring(zb, j, size, send, peer):
         ref = piece(zb * CORES + c, j, size)
@@ -80,9 +127,10 @@
         def _():
             act(j, chunk)
 
-        @pl.when(j == mains)
-        def _():
-            act(mains, tail)
+        for k, span in enumerate(late):
+            @pl.when(j == mains + k)
+            def _(k=k, span=span):
+                act(mains + k, span)
 
     def send(zb, j, size, leftward, rightward):
         @pl.when(jnp.logical_and(leftward, z > 0))
@@ -189,13 +237,6 @@
         sized(t, own)
         sized(t - chips, complete)
 
-        for panel in range(1, panels):
-            @pl.when(jnp.logical_and(t == chips - 1 + panel, a == panel))
-            def _(panel=panel):
-                for before in range(panel):
-                    spread(before, 1).wait_recv()
-                settle(panel)
-
         @pl.when(t == first)
         def _():
             rest_load.wait()
@@ -208,23 +249,24 @@
         for step in range(1, chips):
             sized(t - WINDOW - step, functools.partial(passed, step))
             sized(t - step, functools.partial(pass_on, step))
+        for panel in range(panels):
+            @pl.when(jnp.logical_and(t == (chips - 1 + panel if panel else 2), a == panel))
+            def _(panel=panel):
+                for before in range(panel):
+                    spread(before, 1).wait_recv()
+                settle(panel)
         return 0
 
     own(jnp.int32(0), chunk)
     body_load.wait()
     tail_load.wait()
     rest_load.start()
-    ltail[me, :, :, pl.ds(0, rows - whole)] = ebuf[...]
+    pack(ebuf, ltail, me)
     own(jnp.int32(1), chunk)
+    for step in range(1, chips):
+        sized(jnp.int32(1 - step), functools.partial(pass_on, step))
     pivot_load.wait()
     inverse_load.wait()
-
-    @pl.when(a == 0)
-    def _():
-        settle(0)
-
-    for step in range(1, chips):
-        sized(jnp.int32(1 - step), functools.partial(pass_on, step))
     lax.fori_loop(2, last, tick, 0)
 
     def drain(t, _):
@@ -243,7 +285,8 @@
 
 def write_kernel(chunk, mbuf, sbuf, ltail, out_hbm, solved_hbm, tbuf, out_sem, tail_sem, s_sem):
     rows = mbuf.shape[0]
-    panels = sbuf.shape[0]
+    panels, width = sbuf.shape[:2]
+    pair = ltail.shape[0]
     mains = out_sem.shape[0]
     whole = mains * chunk
 
@@ -255,28 +298,43 @@
     solved = pltpu.make_async_copy(sbuf, solved_hbm, s_sem)
     solved.start()
 
-    def product(here, size):
-        return sum(
+    left = rows - whole
+    part = width // pair
+    groups = panels * part // SUBLANES
+    tiles, ragged, fit = packing(left, groups)
+
+    def store(at, total):
+        here = pl.ds(at, total.shape[0])
+        held = mbuf[pl.ds(whole + at, total.shape[0])].astype(jnp.float32)
+        tbuf[here] = (held - total).astype(jnp.bfloat16)
+
+    def lanes_of(panel, i):
+        return ltail[:, pl.ds((i * panels + panel) * part, part)].reshape(width, LANES)
+
+    for i in range(0, tiles, TILE // LANES):
+        both = range(i, min(tiles, i + TILE // LANES))
+        store(i * LANES, sum(
             lax.dot_general(
-                ltail[:, panel, :, here].reshape(-1, size), sbuf[panel], CONTRACT,
+                jnp.concatenate([lanes_of(panel, i) for i in both], axis=1), sbuf[panel], CONTRACT,
                 preferred_element_type=jnp.float32)
-            for panel in range(panels))
-
-    left = rows - whole
-    full = left // TILE
-    for i in range(full):
-        here = pl.ds(i * TILE, TILE)
-        total = mbuf[pl.ds(whole + i * TILE, TILE)].astype(jnp.float32) - product(here, TILE)
-        tbuf[here] = total.astype(jnp.bfloat16)
-    if left % TILE:
-        here = pl.ds(full * TILE, left % TILE)
-        size = min(-(-(left % TILE) // LANES) * LANES, ltail.shape[-1] - full * TILE)
-        total = product(pl.ds(full * TILE, size), size)[:left % TILE]
-        total = mbuf[pl.ds(whole + full * TILE, left % TILE)].astype(jnp.float32) - total
-        tbuf[here] = total.astype(jnp.bfloat16)
+            for panel in range(panels)))
+    if ragged:
+        base = panels * tiles * part
+        total = 0.0
+        for g in range(groups):
+            slot, off = g // fit, g % fit * ragged
+            panel, at = g * SUBLANES // part, g * SUBLANES % part
+            packed = ltail[:, pl.ds(base + slot * SUBLANES, SUBLANES)].reshape(-1, LANES)
+            solved_rows = sbuf[panel].reshape(pair, part, -1)[:, at:at + SUBLANES]
+            total = total + lax.dot_general(
+                packed, solved_rows.reshape(pair * SUBLANES, -1), CONTRACT,
+                preferred_element_type=jnp.float32)[off:off + ragged]
+        store(tiles * LANES, total)
     final = pltpu.make_async_copy(tbuf, out_hbm.at[pl.ds(whole, left)], tail_sem)
-    lax.fori_loop(0, mains, lambda j, _: (main(j).wait(), 0)[1], 0)
+    early = mains // 2
+    lax.fori_loop(0, early, lambda j, _: (main(j).wait(), 0)[1], 0)
     final.start()
+    lax.fori_loop(early, mains, lambda j, _: (main(j).wait(), 0)[1], 0)
     solved.wait()
     final.wait()
 
@@ -286,11 +344,10 @@
     rows, columns = m_panels.shape
     part = lower_cols.shape[1]
     chips = pair // CORES
-    padded = -(-rows // LANES) * LANES
     chunk = max(CHUNK, -(-width // TILE) * TILE)
-    mains = (rows - 1) // chunk
-    tail = padded - mains * chunk
-    pieces = mains + 1
+    mains = (rows - 1) // chunk - LATE
+    left = rows - mains * chunk
+    pieces = mains + len(late_pieces(chunk, panels, part, left))
     anywhere = pl.BlockSpec(memory_space=pl.ANY)
     vmem = pl.BlockSpec(memory_space=pltpu.VMEM)
     dma = pltpu.SemaphoreType.DMA
@@ -301,11 +358,11 @@
         out_shape=[
             pltpu.VMEM((rows, columns), jnp.bfloat16),
             pltpu.VMEM((panels, width, columns), jnp.bfloat16),
-            pltpu.VMEM((pair, panels, part, tail), jnp.bfloat16),
+            pltpu.VMEM((pair, tail_rows(panels, part, left), LANES), jnp.bfloat16),
         ],
         scratch_shapes=[
             pltpu.VMEM((pair, panels, part, mains * chunk), jnp.bfloat16),
-            pltpu.VMEM((panels, part, rows - mains * chunk), jnp.bfloat16),
+            pltpu.VMEM((panels, part, left), jnp.bfloat16),
             pltpu.VMEM((panels, width, width), jnp.float32),
             dma((6,)),
             dma((chips, pieces)),
@@ -328,7 +385,7 @@
             jax.ShapeDtypeStruct((panels, width, columns), jnp.bfloat16),
         ],
         scratch_shapes=[
-            pltpu.VMEM((rows - mains * chunk, columns), jnp.bfloat16),
+            pltpu.VMEM((left, columns), jnp.bfloat16),
             dma((mains,)),
             dma,
             dma,

time: 185 us -> 183 us (0.989)
  Pallas kernels: 182 us -> 180 us
    pallas_call x1, Pallas kernels: 174 us -> 172 us  [shards(): pl.pallas_call(functools.partial(gather_kernel, aux, chips, chunk), in_sp...]
where the time goes in v2:
time: 183 us; the launch traced here: 180 us
  Pallas kernels  180 us (98%)
    pallas_call x1, Pallas kernels, shards(): pl.pallas_call(functools.partial(gather_kernel, aux, chips, chunk), in_sp...  172 us
    pallas_call x1, Pallas kernels, shards(): pl.pallas_call(functools.partial(write_kernel, chunk), in_specs=[vmem, vm...  7.73 us

profile of v2, /device:TPU:3, one launch (start us, length us, event | category | flops | bytes accessed | tf_op | source)
XLA Modules:
  0.0 180.4 jit_solution(16026610589611595158)
XLA Ops:
  0.6 172.0 %shard_map.50 = (bf16[10000,1024]{1,0:T(8,128)(2,1)S(1)}, bf16[2,512,1024]{2,1,0:T(8,128)(2,1)S(1)}, bf16[8,1808,128]{2,1,0:T(8,128)(2,1)S(1)}) custom-call(bf16[10000,1024]{1,0:T(8,128)(2,1)} %m_hbm.1, bf16[2,64,10000]{2,1,0:T(8,128)(2,1)} %l_hbm.1, f32[2,512,512]{2,1,0:T(8,128)} %d_hbm.1), custom_call_target="tpu_custom_call" | custom-call | tf_op jit(solution)/shard_map/pallas_call | solution.py:354
  172.6 7.7 %shard_map.51 = (bf16[10000,1024]{1,0:T(8,128)(2,1)}, bf16[2,512,1024]{2,1,0:T(8,128)(2,1)}) custom-call(bf16[10000,1024]{1,0:T(8,128)(2,1)S(1)} %get-tuple-element.5.mbuf, bf16[2,512,1024]{2,1,0:T(8,128)(2,1)S(1)} %get-tuple-element.6.sbuf, bf16[8,1808,128]{2,1,0:T(8,128)(2,1)S(1)} %get-tuple-element.7.ltail), custom_call_target="tpu_custom_call" | custom-call | tf_op jit(solution)/shard_map/pallas_call | solution.py:379

commit v3 on v2

--- a/solution.py
+++ b/solution.py
@@ -108,6 +108,8 @@
     def piece(block, j, size):
         if size == chunk:
             return lbuf.at[block, :, :, pl.ds(pl.multiple_of(j * chunk, LANES), chunk)]
+        if size is None:
+            return lbuf.at[block, :, :, pl.ds(width, chunk - width)]
         return ltail.at[block, pl.ds(*size)]
 
     def ring(zb, j, size, send, peer):
@@ -123,9 +125,15 @@
             device_id=partner, device_id_type=MESH)
 
     def sized(j, act):
-        @pl.when(jnp.logical_and(j >= 0, j < mains))
+        bare = jnp.logical_and(j == 0, a == 0)
+
+        @pl.when(jnp.logical_and(jnp.logical_not(bare), jnp.logical_and(j >= 0, j < mains)))
         def _():
             act(j, chunk)
+
+        @pl.when(bare)
+        def _():
+            act(0, None)
 
         for k, span in enumerate(late):
             @pl.when(j == mains + k)
@@ -257,12 +265,17 @@
                 settle(panel)
         return 0
 
-    own(jnp.int32(0), chunk)
+    sized(jnp.int32(0), own)
     body_load.wait()
     tail_load.wait()
     rest_load.start()
     pack(ebuf, ltail, me)
     own(jnp.int32(1), chunk)
+
+    @pl.when(a == 0)
+    def _():
+        lbuf[:, :, :, pl.ds(0, width)] = jnp.zeros(lbuf.shape[:3] + (width,), jnp.bfloat16)
+
     for step in range(1, chips):
         sized(jnp.int32(1 - step), functools.partial(pass_on, step))
     pivot_load.wait()
@@ -344,7 +357,7 @@
     rows, columns = m_panels.shape
     part = lower_cols.shape[1]
     chips = pair // CORES
-    chunk = max(CHUNK, -(-width // TILE) * TILE)
+    chunk = max(CHUNK, (width // TILE + 1) * TILE)
     mains = (rows - 1) // chunk - LATE
     left = rows - mains * chunk
     pieces = mains + len(late_pieces(chunk, panels, part, left))

time: 183 us -> 181 us (0.989); the launches traced: 180 us -> 180 us
  no operation moved by 1% of the time
where the time goes in v3:
time: 181 us; the launch traced here: 180 us
  Pallas kernels  180 us (99%)
    pallas_call x1, Pallas kernels, shards(): pl.pallas_call(functools.partial(gather_kernel, aux, chips, chunk), in_sp...  172 us
    pallas_call x1, Pallas kernels, shards(): pl.pallas_call(functools.partial(write_kernel, chunk), in_specs=[vmem, vm...  7.73 us

profile of v3, /device:TPU:3, one launch (start us, length us, event | category | flops | bytes accessed | tf_op | source)
XLA Modules:
  0.0 180.4 jit_solution(7561276010030304788)
XLA Ops:
  0.6 172.0 %shard_map.50 = (bf16[10000,1024]{1,0:T(8,128)(2,1)S(1)}, bf16[2,512,1024]{2,1,0:T(8,128)(2,1)S(1)}, bf16[8,1808,128]{2,1,0:T(8,128)(2,1)S(1)}) custom-call(bf16[10000,1024]{1,0:T(8,128)(2,1)} %m_hbm.1, bf16[2,64,10000]{2,1,0:T(8,128)(2,1)} %l_hbm.1, f32[2,512,512]{2,1,0:T(8,128)} %d_hbm.1), custom_call_target="tpu_custom_call" | custom-call | tf_op jit(solution)/shard_map/pallas_call | solution.py:367
  172.6 7.7 %shard_map.51 = (bf16[10000,1024]{1,0:T(8,128)(2,1)}, bf16[2,512,1024]{2,1,0:T(8,128)(2,1)}) custom-call(bf16[10000,1024]{1,0:T(8,128)(2,1)S(1)} %get-tuple-element.5.mbuf, bf16[2,512,1024]{2,1,0:T(8,128)(2,1)S(1)} %get-tuple-element.6.sbuf, bf16[8,1808,128]{2,1,0:T(8,128)(2,1)S(1)} %get-tuple-element.7.ltail), custom_call_target="tpu_custom_call" | custom-call | tf_op jit(solution)/shard_map/pallas_call | solution.py:392

commit v4 on v2

--- a/solution.py
+++ b/solution.py
@@ -13,6 +13,8 @@
 LANES = 128
 SUBLANES = 16
 CORES = 2
+CUT = 1
+HOPS = (2, 5, 6)
 WINDOW = 2
 CONTRACT = (((0,), (0,)), ((), ()))
 MESH = pl.DeviceIdType.MESH
@@ -62,9 +64,9 @@
         ltail[me, pl.ds(base + slot * SUBLANES, SUBLANES)] = total.astype(jnp.bfloat16)
 
 
-def gather_kernel(aux, chips, chunk, m_hbm, l_hbm, d_hbm, mbuf, sbuf, ltail,
-                  lbuf, ebuf, dbuf, load_sem, ring_sem, swap_sem, left_sem, right_sem, part_sem,
-                  srecv_sem, ssend_sem):
+def gather_kernel(aux, chips, chunk, cut_at, m_hbm, l_hbm, d_hbm, mbuf, sbuf, ltail,
+                  lbuf, ebuf, dbuf, rbuf, load_sem, ring_sem, swap_sem, left_sem, right_sem, part_sem,
+                  srecv_sem, ssend_sem, hop_sem, relay_sem):
     rows, columns = m_hbm.shape
     panels, width = d_hbm.shape[:2]
     whole = lbuf.shape[-1]
@@ -72,6 +74,8 @@
     left = rows - whole
     late = late_pieces(chunk, panels, l_hbm.shape[1], left)
     pieces = mains + len(late)
+    edge_at = pieces + 1
+    detours = rbuf.shape[0]
     a = lax.axis_index("aux")
     me = lax.axis_index("pair")
     z, c = me // CORES, lax.rem(me, CORES)
@@ -105,10 +109,19 @@
     pl.semaphore_wait(barrier, 2 + aux)
     head_load.wait()
 
-    def piece(block, j, size):
-        if size == chunk:
-            return lbuf.at[block, :, :, pl.ds(pl.multiple_of(j * chunk, LANES), chunk)]
-        return ltail.at[block, pl.ds(*size)]
+    def piece(block, j, kind):
+        name, *span = kind
+        if name == "late":
+            return ltail.at[block, pl.ds(*span)]
+        if name == "head":
+            return lbuf.at[block, pl.ds(0, *span), :, pl.ds(0, width)]
+        if name == "bare":
+            return lbuf.at[block, :, :, pl.ds(width, chunk - width)]
+        if name == "edge":
+            return lbuf.at[block, :, :, pl.ds((cut_at + 1) * chunk - LANES, LANES)]
+        if name == "cut":
+            return lbuf.at[block, :, :, pl.ds(cut_at * chunk, chunk - LANES)]
+        return lbuf.at[block, :, :, pl.ds(pl.multiple_of(j * chunk, LANES), chunk)]
 
     def ring(zb, j, size, send, peer):
         ref = piece(zb * CORES + c, j, size)
@@ -123,36 +136,145 @@
             device_id=partner, device_id_type=MESH)
 
     def sized(j, act):
-        @pl.when(jnp.logical_and(j >= 0, j < mains))
-        def _():
-            act(j, chunk)
+        whole_piece = jnp.logical_or(j > 0, a >= panels)
+        whole_piece = jnp.logical_and(whole_piece, jnp.logical_and(j >= 0, j < mains))
+        whole_piece = jnp.logical_and(whole_piece, j != cut_at)
+
+        @pl.when(whole_piece)
+        def _():
+            act(j, ("main",))
+
+        for block in range(panels):
+            @pl.when(jnp.logical_and(j == 0, a == block))
+            def _(block=block):
+                act(0, ("bare",))
+                if block:
+                    act(pieces, ("head", block))
+
+        @pl.when(j == cut_at)
+        def _():
+            act(edge_at, ("edge",))
+            act(cut_at, ("cut",))
 
         for k, span in enumerate(late):
             @pl.when(j == mains + k)
             def _(k=k, span=span):
-                act(mains + k, span)
+                act(mains + k, ("late", *span))
+
+    detoured = jnp.logical_and(a >= panels, a < panels + detours)
+    lane = jnp.clip(a - panels, 0, max(detours - 1, 0))
+
+    def via(zb, send):
+        return pltpu.make_async_remote_copy(
+            src_ref=piece(zb * CORES + c, edge_at, ("edge",)), dst_ref=rbuf.at[lane, zb],
+            send_sem=send.at[zb, edge_at], recv_sem=hop_sem.at[0, lane, zb],
+            device_id={"aux": 0}, device_id_type=MESH)
+
+    def along(d, zb, peer):
+        return pltpu.make_async_remote_copy(
+            src_ref=rbuf.at[d, zb], dst_ref=rbuf.at[d, zb],
+            send_sem=relay_sem.at[d, zb], recv_sem=hop_sem.at[1, d, zb],
+            device_id=peer, device_id_type=MESH)
+
+    def back(d, zb):
+        return pltpu.make_async_remote_copy(
+            src_ref=rbuf.at[d, zb], dst_ref=piece(zb * CORES + c, edge_at, ("edge",)),
+            send_sem=relay_sem.at[d, zb], recv_sem=ring_sem.at[zb, edge_at],
+            device_id={"aux": panels + d}, device_id_type=MESH)
+
+    sides = ((0, 1, 1, to_left), (chips - 1, chips - 2, -1, to_right)) if detours else ()
+
+    def hops(t):
+        for end, near, sign, peer in sides:
+            for d in range(detours):
+                s = t - cut_at - HOPS[0]
+
+                @pl.when(jnp.logical_and(a == 0, jnp.logical_and(
+                    z == near, jnp.logical_and(s >= 0, s < chips - 1))))
+                def _(s=s, d=d, near=near, sign=sign, peer=peer):
+                    zb = near + sign * s
+                    pltpu.make_async_remote_copy(
+                        src_ref=rbuf.at[d, zb], dst_ref=rbuf.at[d, zb],
+                        send_sem=relay_sem.at[d, zb], recv_sem=hop_sem.at[0, d, zb],
+                        device_id=peer, device_id_type=MESH).wait_recv()
+                    along(d, zb, peer).start()
+
+                s = t - cut_at - HOPS[1]
+
+                @pl.when(jnp.logical_and(a == 0, jnp.logical_and(
+                    z == end, jnp.logical_and(s >= 0, s < chips - 1))))
+                def _(s=s, d=d, near=near, sign=sign, peer=peer):
+                    zb = near + sign * s
+                    along(d, zb, peer).wait_recv()
+                    back(d, zb).start()
+
+            s = t - cut_at - HOPS[2]
+
+            @pl.when(jnp.logical_and(detoured, jnp.logical_and(
+                z == end, jnp.logical_and(s >= 0, s < chips - 1))))
+            def _(s=s, near=near, sign=sign, peer=peer):
+                zb = near + sign * s
+                ring(zb, edge_at, ("edge",), left_sem, peer).wait_recv()
+                swap(zb, edge_at, ("edge",), c).start()
+
+    def hops_sent():
+        for end, near, sign, peer in sides:
+            def relayed(s, _, end=end, near=near, sign=sign, peer=peer):
+                zb = near + sign * s
+                for d in range(detours):
+                    @pl.when(jnp.logical_and(a == 0, z == near))
+                    def _(d=d):
+                        along(d, zb, peer).wait_send()
+
+                    @pl.when(jnp.logical_and(a == 0, z == end))
+                    def _(d=d):
+                        back(d, zb).wait_send()
+
+                @pl.when(jnp.logical_and(detoured, z == end))
+                def _():
+                    swap(zb, edge_at, ("edge",), c).wait_send()
+                return 0
+
+            lax.fori_loop(0, chips - 1, relayed, 0)
+
+    def leave(zb, j, size, leftward, rightward, act):
+        goes_left = jnp.logical_and(leftward, z > 0)
+        goes_right = jnp.logical_and(rightward, z < chips - 1)
+        if size[0] == "edge" and detours:
+            round_left = jnp.logical_and(goes_left, jnp.logical_and(detoured, z == 1))
+            round_right = jnp.logical_and(goes_right, jnp.logical_and(detoured, z == chips - 2))
+            goes_left = jnp.logical_and(goes_left, jnp.logical_not(round_left))
+            goes_right = jnp.logical_and(goes_right, jnp.logical_not(round_right))
+
+            @pl.when(round_left)
+            def _():
+                act(via(zb, left_sem))
+
+            @pl.when(round_right)
+            def _():
+                act(via(zb, right_sem))
+
+        @pl.when(goes_left)
+        def _():
+            act(ring(zb, j, size, left_sem, to_left))
+
+        @pl.when(goes_right)
+        def _():
+            act(ring(zb, j, size, right_sem, to_right))
+
+        act(swap(zb, j, size, c))
 
     def send(zb, j, size, leftward, rightward):
-        @pl.when(jnp.logical_and(leftward, z > 0))
-        def _():
-            ring(zb, j, size, left_sem, to_left).start()
-
-        @pl.when(jnp.logical_and(rightward, z < chips - 1))
-        def _():
-            ring(zb, j, size, right_sem, to_right).start()
-
-        swap(zb, j, size, c).start()
+        leave(zb, j, size, leftward, rightward, lambda copy: copy.start())
 
     def sent(zb, j, size, leftward, rightward):
-        @pl.when(jnp.logical_and(leftward, z > 0))
-        def _():
-            ring(zb, j, size, left_sem, to_left).wait_send()
-
-        @pl.when(jnp.logical_and(rightward, z < chips - 1))
-        def _():
-            ring(zb, j, size, right_sem, to_right).wait_send()
-
-        swap(zb, j, size, c).wait_send()
+        leave(zb, j, size, leftward, rightward, lambda copy: copy.wait_send())
+
+    def arrives(zb, size, end):
+        here = jnp.logical_and(zb >= 0, zb < chips)
+        if size[0] == "edge" and detours:
+            here = jnp.logical_and(here, jnp.logical_not(jnp.logical_and(detoured, z == end)))
+        return here
 
     def own(j, size):
         send(z, j, size, True, True)
@@ -161,26 +283,28 @@
         sent(z, j, size, True, True)
 
     def pass_on(step, j, size):
-        @pl.when(z + step < chips)
+        @pl.when(arrives(z + step, size, 0))
         def _():
             ring(z + step, j, size, left_sem, to_left).wait_recv()
             send(z + step, j, size, True, False)
 
-        @pl.when(z >= step)
+        @pl.when(arrives(z - step, size, chips - 1))
         def _():
             ring(z - step, j, size, right_sem, to_right).wait_recv()
             send(z - step, j, size, False, True)
 
     def passed(step, j, size):
-        @pl.when(z + step < chips)
+        @pl.when(arrives(z + step, size, 0))
         def _():
             sent(z + step, j, size, True, False)
 
-        @pl.when(z >= step)
+        @pl.when(arrives(z - step, size, chips - 1))
         def _():
             sent(z - step, j, size, False, True)
 
     def complete(j, size):
+        if size[0] == "edge":
+            return
         for zb in range(chips):
             swap(zb, j, size, 1 - c).wait_recv()
 
@@ -210,7 +334,12 @@
         for step in range(1, aux):
             spread(panel, step).start()
 
+    before_last = max(mains - 2, cut_at)
+
     def update(j, _):
+        at = jnp.where(jnp.logical_or(j < cut_at, j == mains - 1), j, j + 1)
+        at = jnp.where(j == before_last, cut_at, at)
+
         def tile(i, _):
             here = pl.ds(pl.multiple_of(i * TILE, TILE), TILE)
             product = sum(
@@ -222,20 +351,28 @@
             return 0
 
         tiles = chunk // TILE
-        lax.fori_loop(j * tiles, (j + 1) * tiles, tile, 0)
+        lax.fori_loop(at * tiles, (at + 1) * tiles, tile, 0)
         return 0
 
-    last = pieces + chips
+    edges_in = cut_at + HOPS[2] + chips - 1
+    last = max(pieces + chips, edges_in + 1)
     first = min(chips + panels + 1, last - 1 - (mains + 1) // 2)
 
     def done_by(t):
-        ready = jnp.minimum(t - chips + 1, 2 * (t - first + 1))
+        ready = jnp.where(t >= max(edges_in, before_last + chips), t - chips + 1,
+                          jnp.minimum(t - chips, before_last))
+        ready = jnp.minimum(ready, 2 * (t - first + 1))
         return jnp.clip(jnp.where(t == last - 1, mains, ready), 0, mains)
 
     def tick(t, _):
         sized(t - WINDOW, own_sent)
         sized(t, own)
         sized(t - chips, complete)
+
+        @pl.when(t == edges_in)
+        def _():
+            for zb in range(chips):
+                swap(zb, edge_at, ("edge",), 1 - c).wait_recv()
 
         @pl.when(t == first)
         def _():
@@ -249,6 +386,7 @@
         for step in range(1, chips):
             sized(t - WINDOW - step, functools.partial(passed, step))
             sized(t - step, functools.partial(pass_on, step))
+        hops(t)
         for panel in range(panels):
             @pl.when(jnp.logical_and(t == (chips - 1 + panel if panel else 2), a == panel))
             def _(panel=panel):
@@ -257,12 +395,19 @@
                 settle(panel)
         return 0
 
-    own(jnp.int32(0), chunk)
+    sized(jnp.int32(0), own)
     body_load.wait()
     tail_load.wait()
     rest_load.start()
     pack(ebuf, ltail, me)
-    own(jnp.int32(1), chunk)
+    sized(jnp.int32(1), own)
+
+    for block in range(panels):
+        @pl.when(a == block)
+        def _(block=block):
+            shape = (lbuf.shape[0], panels - block, lbuf.shape[2], width)
+            lbuf[:, pl.ds(block, panels - block), :, pl.ds(0, width)] = jnp.zeros(shape, jnp.bfloat16)
+
     for step in range(1, chips):
         sized(jnp.int32(1 - step), functools.partial(pass_on, step))
     pivot_load.wait()
@@ -276,6 +421,7 @@
         return 0
 
     lax.fori_loop(last, last + WINDOW, drain, 0)
+    hops_sent()
     for panel in range(panels):
         @pl.when(a == panel)
         def _(panel=panel):
@@ -344,15 +490,17 @@
     rows, columns = m_panels.shape
     part = lower_cols.shape[1]
     chips = pair // CORES
-    chunk = max(CHUNK, -(-width // TILE) * TILE)
+    chunk = max(CHUNK, (width // TILE + 1) * TILE)
     mains = (rows - 1) // chunk - LATE
     left = rows - mains * chunk
     pieces = mains + len(late_pieces(chunk, panels, part, left))
+    cut_at = min(CUT, mains - 1)
+    detours = min(panels, aux - panels) if chips >= 4 else 0
     anywhere = pl.BlockSpec(memory_space=pl.ANY)
     vmem = pl.BlockSpec(memory_space=pltpu.VMEM)
     dma = pltpu.SemaphoreType.DMA
     held, solved, ltail = pl.pallas_call(
-        functools.partial(gather_kernel, aux, chips, chunk),
+        functools.partial(gather_kernel, aux, chips, chunk, cut_at),
         in_specs=[anywhere, anywhere, anywhere],
         out_specs=[vmem, vmem, vmem],
         out_shape=[
@@ -364,14 +512,17 @@
             pltpu.VMEM((pair, panels, part, mains * chunk), jnp.bfloat16),
             pltpu.VMEM((panels, part, left), jnp.bfloat16),
             pltpu.VMEM((panels, width, width), jnp.float32),
+            pltpu.VMEM((detours, chips, panels, part, LANES), jnp.bfloat16),
             dma((6,)),
-            dma((chips, pieces)),
-            dma((chips, pieces)),
-            dma((chips, pieces)),
-            dma((chips, pieces)),
-            dma((chips, pieces)),
+            dma((chips, pieces + 2)),
+            dma((chips, pieces + 2)),
+            dma((chips, pieces + 2)),
+            dma((chips, pieces + 2)),
+            dma((chips, pieces + 2)),
             dma((panels,)),
             dma((panels, aux)),
+            dma((2, max(detours, 1), chips)),
+            dma((max(detours, 1), chips)),
         ],
         compiler_params=pltpu.CompilerParams(
             collective_id=0, has_side_effects=True, vmem_limit_bytes=36 * 1024 * 1024),

time: 183 us -> 179 us (0.978)
  Pallas kernels: 180 us -> 176 us
    pallas_call x1, Pallas kernels: 172 us -> 169 us  [shards(): pl.pallas_call(functools.partial(gather_kernel, aux, chips, chunk, cut_at...]
where the time goes in v4:
time: 179 us; the launch traced here: 177 us
  Pallas kernels  176 us (98%)
    pallas_call x1, Pallas kernels, shards(): pl.pallas_call(functools.partial(gather_kernel, aux, chips, chunk, cut_at...  169 us
    pallas_call x1, Pallas kernels, shards(): pl.pallas_call(functools.partial(write_kernel, chunk), in_specs=[vmem, vm...  7.73 us

profile of v4, /device:TPU:3, one launch (start us, length us, event | category | flops | bytes accessed | tf_op | source)
XLA Modules:
  0.0 177.1 jit_solution(852498572738709409)
XLA Ops:
  0.6 168.7 %shard_map.50 = (bf16[10000,1024]{1,0:T(8,128)(2,1)S(1)}, bf16[2,512,1024]{2,1,0:T(8,128)(2,1)S(1)}, bf16[8,1808,128]{2,1,0:T(8,128)(2,1)S(1)}) custom-call(bf16[10000,1024]{1,0:T(8,128)(2,1)} %m_hbm.1, bf16[2,64,10000]{2,1,0:T(8,128)(2,1)} %l_hbm.1, f32[2,512,512]{2,1,0:T(8,128)} %d_hbm.1), custom_call_target="tpu_custom_call" | custom-call | tf_op jit(solution)/shard_map/pallas_call | solution.py:502
  169.4 7.7 %shard_map.51 = (bf16[10000,1024]{1,0:T(8,128)(2,1)}, bf16[2,512,1024]{2,1,0:T(8,128)(2,1)}) custom-call(bf16[10000,1024]{1,0:T(8,128)(2,1)S(1)} %get-tuple-element.5.mbuf, bf16[2,512,1024]{2,1,0:T(8,128)(2,1)S(1)} %get-tuple-element.6.sbuf, bf16[8,1808,128]{2,1,0:T(8,128)(2,1)S(1)} %get-tuple-element.7.ltail), custom_call_target="tpu_custom_call" | custom-call | tf_op jit(solution)/shard_map/pallas_call | solution.py:530

commit v5 on v4

--- a/solution.py
+++ b/solution.py
@@ -15,6 +15,7 @@
 CORES = 2
 CUT = 1
 HOPS = (2, 5, 6)
+ENDING = 4
 WINDOW = 2
 CONTRACT = (((0,), (0,)), ((), ()))
 MESH = pl.DeviceIdType.MESH
@@ -121,7 +122,8 @@
             return lbuf.at[block, :, :, pl.ds((cut_at + 1) * chunk - LANES, LANES)]
         if name == "cut":
             return lbuf.at[block, :, :, pl.ds(cut_at * chunk, chunk - LANES)]
-        return lbuf.at[block, :, :, pl.ds(pl.multiple_of(j * chunk, LANES), chunk)]
+        at = j * chunk if isinstance(j, int) else pl.multiple_of(j * chunk, LANES)
+        return lbuf.at[block, :, :, pl.ds(at, chunk)]
 
     def ring(zb, j, size, send, peer):
         ref = piece(zb * CORES + c, j, size)
@@ -136,6 +138,17 @@
             device_id=partner, device_id_type=MESH)
 
     def sized(j, act):
+        if isinstance(j, int) and j > 0:
+            if j == cut_at:
+                act(edge_at, ("edge",))
+                act(cut_at, ("cut",))
+            elif j < mains:
+                act(j, ("main",))
+            elif j < pieces:
+                act(j, ("late", *late[j - mains]))
+            return
+        if isinstance(j, int) and j < 0:
+            return
         whole_piece = jnp.logical_or(j > 0, a >= panels)
         whole_piece = jnp.logical_and(whole_piece, jnp.logical_and(j >= 0, j < mains))
         whole_piece = jnp.logical_and(whole_piece, j != cut_at)
@@ -359,48 +372,62 @@
     first = min(chips + panels + 1, last - 1 - (mains + 1) // 2)
 
     def done_by(t):
+        if isinstance(t, int):
+            ready = t - chips + 1
+            if t < max(edges_in, before_last + chips):
+                ready = min(t - chips, before_last)
+            ready = mains if t == last - 1 else min(ready, 2 * (t - first + 1))
+            return max(0, min(ready, mains))
         ready = jnp.where(t >= max(edges_in, before_last + chips), t - chips + 1,
                           jnp.minimum(t - chips, before_last))
         ready = jnp.minimum(ready, 2 * (t - first + 1))
         return jnp.clip(jnp.where(t == last - 1, mains, ready), 0, mains)
 
-    def tick(t, _):
-        sized(t - WINDOW, own_sent)
-        sized(t, own)
-        sized(t - chips, complete)
-
-        @pl.when(t == edges_in)
-        def _():
-            for zb in range(chips):
-                swap(zb, edge_at, ("edge",), 1 - c).wait_recv()
-
-        @pl.when(t == first)
-        def _():
-            rest_load.wait()
-            for panel in range(panels):
-                @pl.when(jnp.logical_and(a != panel, jnp.logical_or(a < panel, a >= panels)))
-                def _(panel=panel):
-                    spread(panel, 1).wait_recv()
-
-        lax.fori_loop(done_by(t - 1), done_by(t), update, 0)
-        for step in range(1, chips):
-            sized(t - WINDOW - step, functools.partial(passed, step))
-            sized(t - step, functools.partial(pass_on, step))
-        hops(t)
+    def solves(t):
         for panel in range(panels):
             @pl.when(jnp.logical_and(t == (chips - 1 + panel if panel else 2), a == panel))
             def _(panel=panel):
                 for before in range(panel):
                     spread(before, 1).wait_recv()
                 settle(panel)
+
+    def joins(t):
+        @pl.when(t == 4)
+        def _():
+            rest_load.start()
+
+        @pl.when(t == edges_in)
+        def _():
+            for zb in range(chips):
+                swap(zb, edge_at, ("edge",), 1 - c).wait_recv()
+
+        @pl.when(t == first)
+        def _():
+            rest_load.wait()
+            for panel in range(panels):
+                @pl.when(jnp.logical_and(a != panel, jnp.logical_or(a < panel, a >= panels)))
+                def _(panel=panel):
+                    spread(panel, 1).wait_recv()
+
+    def tick(t, _):
+        sized(t - WINDOW, own_sent)
+        sized(t, own)
+        sized(t - chips, complete)
+        joins(t)
+        lax.fori_loop(done_by(t - 1), done_by(t), update, 0)
+        for step in range(1, chips):
+            sized(t - WINDOW - step, functools.partial(passed, step))
+            sized(t - step, functools.partial(pass_on, step))
+        if not isinstance(t, int):
+            hops(t)
+            solves(t)
         return 0
 
-    sized(jnp.int32(0), own)
+    sized(0, own)
     body_load.wait()
     tail_load.wait()
-    rest_load.start()
     pack(ebuf, ltail, me)
-    sized(jnp.int32(1), own)
+    sized(1, own)
 
     for block in range(panels):
         @pl.when(a == block)
@@ -409,18 +436,19 @@
             lbuf[:, pl.ds(block, panels - block), :, pl.ds(0, width)] = jnp.zeros(shape, jnp.bfloat16)
 
     for step in range(1, chips):
-        sized(jnp.int32(1 - step), functools.partial(pass_on, step))
+        sized(1 - step, functools.partial(pass_on, step))
     pivot_load.wait()
     inverse_load.wait()
-    lax.fori_loop(2, last, tick, 0)
-
-    def drain(t, _):
+    steady = max(last - ENDING, cut_at + HOPS[2] + chips - 1, chips + panels, first + 1)
+    steady = min(steady, last)
+    lax.fori_loop(2, steady, tick, 0)
+    for t in range(steady, last):
+        tick(t, 0)
+
+    for t in range(last, last + WINDOW):
         sized(t - WINDOW, own_sent)
         for step in range(1, chips):
             sized(t - WINDOW - step, functools.partial(passed, step))
-        return 0
-
-    lax.fori_loop(last, last + WINDOW, drain, 0)
     hops_sent()
     for panel in range(panels):
         @pl.when(a == panel)
@@ -449,10 +477,20 @@
     groups = panels * part // SUBLANES
     tiles, ragged, fit = packing(left, groups)
 
+    stored = []
+
+    def written(k):
+        at, size = stored[k]
+        return pltpu.make_async_copy(
+            tbuf.at[pl.ds(at, size)], out_hbm.at[pl.ds(whole + at, size)], tail_sem.at[k])
+
     def store(at, total):
-        here = pl.ds(at, total.shape[0])
-        held = mbuf[pl.ds(whole + at, total.shape[0])].astype(jnp.float32)
-        tbuf[here] = (held - total).astype(jnp.bfloat16)
+        size = total.shape[0]
+        held = mbuf[pl.ds(whole + at, size)].astype(jnp.float32)
+        tbuf[pl.ds(at, size)] = (held - total).astype(jnp.bfloat16)
+        stored.append((at, size))
+        if len(stored) > 1:
+            written(len(stored) - 2).start()
 
     def lanes_of(panel, i):
         return ltail[:, pl.ds((i * panels + panel) * part, part)].reshape(width, LANES)
@@ -476,13 +514,13 @@
                 packed, solved_rows.reshape(pair * SUBLANES, -1), CONTRACT,
                 preferred_element_type=jnp.float32)[off:off + ragged]
         store(tiles * LANES, total)
-    final = pltpu.make_async_copy(tbuf, out_hbm.at[pl.ds(whole, left)], tail_sem)
     early = mains // 2
     lax.fori_loop(0, early, lambda j, _: (main(j).wait(), 0)[1], 0)
-    final.start()
+    written(len(stored) - 1).start()
     lax.fori_loop(early, mains, lambda j, _: (main(j).wait(), 0)[1], 0)
     solved.wait()
-    final.wait()
+    for k in range(len(stored)):
+        written(k).wait()
 
 
 def shards(aux, pair, m_panels, lower_cols, diag_inverses):
@@ -538,7 +576,7 @@
         scratch_shapes=[
             pltpu.VMEM((left, columns), jnp.bfloat16),
             dma((mains,)),
-            dma,
+            dma((left // TILE + 2,)),
             dma,
         ],
         compiler_params=pltpu.CompilerParams(vmem_limit_bytes=8 * 1024 * 1024),

time: 179 us -> 179 us (level)
  no operation moved by 1% of the time
where the time goes in v5:
time: 179 us; the launch traced here: 177 us
  Pallas kernels  176 us (98%)
    pallas_call x1, Pallas kernels, shards(): pl.pallas_call(functools.partial(gather_kernel, aux, chips, chunk, cut_at...  168 us
    pallas_call x1, Pallas kernels, shards(): pl.pallas_call(functools.partial(write_kernel, chunk), in_specs=[vmem, vm...  7.7 us

profile of v5, /device:TPU:3, one launch (start us, length us, event | category | flops | bytes accessed | tf_op | source)
XLA Modules:
  0.0 176.7 jit_solution(14659471452376345008)
XLA Ops:
  0.6 168.3 %shard_map.50 = (bf16[10000,1024]{1,0:T(8,128)(2,1)S(1)}, bf16[2,512,1024]{2,1,0:T(8,128)(2,1)S(1)}, bf16[8,1808,128]{2,1,0:T(8,128)(2,1)S(1)}) custom-call(bf16[10000,1024]{1,0:T(8,128)(2,1)} %m_hbm.1, bf16[2,64,10000]{2,1,0:T(8,128)(2,1)} %l_hbm.1, f32[2,512,512]{2,1,0:T(8,128)} %d_hbm.1), custom_call_target="tpu_custom_call" | custom-call | tf_op jit(solution)/shard_map/pallas_call | solution.py:540
  169.0 7.7 %shard_map.51 = (bf16[10000,1024]{1,0:T(8,128)(2,1)}, bf16[2,512,1024]{2,1,0:T(8,128)(2,1)}) custom-call(bf16[10000,1024]{1,0:T(8,128)(2,1)S(1)} %get-tuple-element.5.mbuf, bf16[2,512,1024]{2,1,0:T(8,128)(2,1)S(1)} %get-tuple-element.6.sbuf, bf16[8,1808,128]{2,1,0:T(8,128)(2,1)S(1)} %get-tuple-element.7.ltail), custom_call_target="tpu_custom_call" | custom-call | tf_op jit(solution)/shard_map/pallas_call | solution.py:568

commit v6 on v5

--- a/solution.py
+++ b/solution.py
@@ -465,10 +465,11 @@
     whole = mains * chunk
 
     def main(j):
-        here = pl.ds(pl.multiple_of(j * chunk, chunk), chunk)
+        here = pl.ds(j * chunk, chunk)
         return pltpu.make_async_copy(mbuf.at[here], out_hbm.at[here], out_sem.at[j])
 
-    lax.fori_loop(0, mains, lambda j, _: (main(j).start(), 0)[1], 0)
+    for j in range(mains):
+        main(j).start(priority=j % 2)
     solved = pltpu.make_async_copy(sbuf, solved_hbm, s_sem)
     solved.start()
 

time: 179 us -> 179 us (level)
  no operation moved by 1% of the time
where the time goes in v6:
time: 179 us; the launch traced here: 177 us
  Pallas kernels  176 us (98%)
    pallas_call x1, Pallas kernels, shards(): pl.pallas_call(functools.partial(gather_kernel, aux, chips, chunk, cut_at...  168 us
    pallas_call x1, Pallas kernels, shards(): pl.pallas_call(functools.partial(write_kernel, chunk), in_specs=[vmem, vm...  7.76 us

profile of v6, /device:TPU:3, one launch (start us, length us, event | category | flops | bytes accessed | tf_op | source)
XLA Modules:
  0.0 176.7 jit_solution(10533753183997013839)
XLA Ops:
  0.6 168.3 %shard_map.50 = (bf16[10000,1024]{1,0:T(8,128)(2,1)S(1)}, bf16[2,512,1024]{2,1,0:T(8,128)(2,1)S(1)}, bf16[8,1808,128]{2,1,0:T(8,128)(2,1)S(1)}) custom-call(bf16[10000,1024]{1,0:T(8,128)(2,1)} %m_hbm.1, bf16[2,64,10000]{2,1,0:T(8,128)(2,1)} %l_hbm.1, f32[2,512,512]{2,1,0:T(8,128)} %d_hbm.1), custom_call_target="tpu_custom_call" | custom-call | tf_op jit(solution)/shard_map/pallas_call | solution.py:541
  169.0 7.8 %shard_map.51 = (bf16[10000,1024]{1,0:T(8,128)(2,1)}, bf16[2,512,1024]{2,1,0:T(8,128)(2,1)}) custom-call(bf16[10000,1024]{1,0:T(8,128)(2,1)S(1)} %get-tuple-element.5.mbuf, bf16[2,512,1024]{2,1,0:T(8,128)(2,1)S(1)} %get-tuple-element.6.sbuf, bf16[8,1808,128]{2,1,0:T(8,128)(2,1)S(1)} %get-tuple-element.7.ltail), custom_call_target="tpu_custom_call" | custom-call | tf_op jit(solution)/shard_map/pallas_call | solution.py:569
